TPU v7x, 32 devices: a whole 2x2x4 slice. The times are simulated.
32 devices in a mesh: seq: 8 (over z, y), head: 4 (over x, core).
Axes of the slice: x: 2, y: 2, z: 4, core: 2. Of those that a mesh axis runs over, the one named last changes fastest.
Arguments:
- queries: bfloat16 [4096, 2048], P('seq', 'head'), may hold values from -6 to 6
- key_vectors: bfloat16 [4096, 2048], P('seq', 'head'), may hold values from -6 to 6
- value_vectors: bfloat16 [4096, 2048], P('seq', 'head'), may hold values from -6 to 6
- gate_input: bfloat16 [4096, 2048], P('seq', 'head'), may hold values from -6 to 6
- out_weight: bfloat16 [2048, 4096], P('seq', 'head'), may hold values from -0.125 to 0.125
Outputs:
- layer_output: bfloat16 [4096, 4096], P('seq', 'head')
All inputs are finite; a program needn't handle non-finite values.
Results may differ from a plain program's by a relative error of at most 0.0057.
Values may be sent and summed in bfloat16 or wider, within the bound.
A program may use at most 64 MiB of HBM per device.

v0:
```python
import jax
import jax.numpy as jnp
from jax import lax
from jax.sharding import PartitionSpec as P

HD = 128


def carried_in(shard, axis, combine, identity):
    count, position = (lax.axis_size(axis), lax.axis_index(axis))
    everything = lax.all_gather(shard, axis)
    start = jnp.broadcast_to(jnp.asarray(identity, shard.dtype), shard.shape)

    def turn(k, before):
        reached = k < position
        new = combine(before, everything[k])
        return jnp.where(reached, new, before)

    return lax.fori_loop(0, count, turn, start)


def add_states(earlier, later):
    return earlier + later


def carried(own_state):
    return carried_in(own_state, "seq", add_states, jnp.zeros_like(own_state))


def in_shard(qhead, khead, vhead, scale):
    rows = qhead.shape[0]
    step = min(rows, 512)
    scores = jnp.einsum("thd,shd->hts", qhead, khead, preferred_element_type=jnp.float32) * scale
    rowpos = 0 + lax.broadcasted_iota(jnp.int32, (step, step), 0)
    colpos = lax.broadcasted_iota(jnp.int32, (step, step), 1)
    scores = jnp.where((colpos <= rowpos)[None, :, :], scores, 0.0).astype(jnp.bfloat16)
    pieces = jnp.einsum("hts,she->the", scores, vhead, preferred_element_type=jnp.float32)
    return pieces


def per_device(queries, key_vectors, value_vectors, gate_input, out_weight):
    rows, width = queries.shape
    heads = width // HD
    scale = HD ** (-0.5)
    qhead = queries.reshape(rows, heads, HD)
    khead = key_vectors.reshape(rows, heads, HD)
    vhead = value_vectors.reshape(rows, heads, HD)
    own_state = jnp.einsum("thd,the->hde", khead, vhead, preferred_element_type=jnp.float32)
    local = in_shard(qhead, khead, vhead, scale)
    prefix = carried(own_state)
    inter = (
        jnp.einsum(
            "thd,hde->the", qhead, prefix.astype(jnp.bfloat16), preferred_element_type=jnp.float32
        )
        * scale
    )
    attn = (local + inter).reshape(rows, width)
    squares = jnp.sum(attn * attn, axis=1)
    hidden = (attn * jax.nn.silu(gate_input.astype(jnp.float32))).astype(jnp.bfloat16)
    total = lax.psum(squares, "head")
    features = lax.all_gather(hidden, "head", axis=1, tiled=True)
    full_block = lax.all_gather(out_weight, "seq", axis=0, tiled=True)
    projected = jnp.dot(features, full_block, preferred_element_type=jnp.float32)
    mean_square = total / features.shape[1]
    return (projected * lax.rsqrt(mean_square + 1e-06)[:, None]).astype(jnp.bfloat16)


def solution(mesh):
    placed = (
        P("seq", "head"),
        P("seq", "head"),
        P("seq", "head"),
        P("seq", "head"),
        P("seq", "head"),
    )
    return jax.shard_map(
        per_device, mesh=mesh, in_specs=placed, out_specs=P("seq", "head"), check_vma=False
    )
```

profile of v0, /device:TPU:0, one launch (start us, length us, event | category | flops | bytes accessed | tf_op | source)
XLA Modules:
  0.0 184.2 jit_solution(1914398323355310470)
XLA Ops:
  6.5 0.0 copy-start
  6.5 0.0 all-gather.9.cloned.1.call-start
  6.5 1.3 copy.19
  7.9 2.0 %fusion.10 = f32[4,128,128]{2,1,0:T(8,128)} fusion(bf16[512,4,128]{0,2,1:T(8,128)(2,1)S(1)} %bitcast.47, bf16[512,512]{1,0:T(8,128)(2,1)} %param.9), kind=kOutput, calls=%fused_computation.18 | convolution fusion | flops 67108864 | bytes 1310720 | tf_op jit(solution)/shard_map/thd,the->hde/dot_general | solution.py:48
  9.9 0.0 all-gather.9.cloned.1.call-update
  9.9 0.0 all-gather.5.cloned.1.call-start
  10.0 0.1 iota_compare_fusion
  10.1 51.8 %all-gather.9.cloned.1.call-done = f32[32,128,128]{2,1,0:T(8,128)} async-done(((f32[4,128,128]{2,1,0:T(8,128)}), f32[32,128,128]{2,1,0:T(8,128)}) %all-gather.9.cloned.1.call-update) | async-done | bytes 2097168 | tf_op jit(solution)/shard_map/all_gather | solution.py:11
  61.9 8.5 %while.14 = (s32[]{:T(128)}, f32[4,128,128]{2,1,0:T(8,128)S(1)}, s32[]{:T(128)}, f32[8,4,128,128]{3,2,1,0:T(8,128)}, s32[]{:T(128)}, /*index=5*/s32[]{:T(128)}) while((s32[]{:T(128)}, f32[4,128,128]{2,1,0:T(8,128)S(1)}, s32[]{:T(128)}, f32[8,4,128,128]{3,2,1,0:T(8,128)}, s32[]{:T(128)}, /*index=5*/s32[]{:T(128)}) %tuple.42), condition=%wide.region_1.2_spmd.clone, body=%wide.region_0.1_spmd.clone.sunk | while | flops 196612 | bytes 786525 | solution.py:19
  61.9 1.0 add_select_fusion.2
  62.9 1.0 add_select_fusion.2
  64.0 1.0 add_select_fusion.2
  65.1 1.0 add_select_fusion.2
  66.1 1.0 add_select_fusion.2
  67.2 1.0 add_select_fusion.2
  68.3 1.0 add_select_fusion.2
  69.3 1.0 add_select_fusion.2
  70.4 0.0 copy-done
  70.4 0.3 fusion.3
  70.7 2.4 %multiply_reduce_fusion = (f32[512]{0:T(512)S(1)}, f32[512,4,128]{0,2,1:T(8,128)S(1)}) fusion(f32[512,4,128]{0,2,1:T(8,128)S(1)} %fusion.3, bf16[512,4,128]{0,2,1:T(8,128)(2,1)S(1)} %bitcast.48, pred[512,512]{1,0:T(8,128)(4,1)S(1)} %iota_compare_fusion, bf16[512,512]{1,0:T(8,128)(2,1)} %param.9, bf16[512,512]{1,0:T(8,128)(2,1)S(1)} %copy-done), kind=kOutput, calls=%fused_computation.14 | convolution fusion | flops 540802560 | bytes 3934208 | tf_op jit(solution)/shard_map/hts,she->the/dot_general | solution.py:37
  73.2 0.0 copy-start.1
  73.2 0.3 copy.17
  73.5 0.7 copy-done.1
  74.2 1.1 fusion.8
  75.3 0.0 all-gather.5.cloned.1.call-update
  75.3 0.0 all-gather.7.cloned.1.call-start
  75.4 0.7 all-gather.7.cloned.1.call-update
  76.1 5.7 %psum.7 = f32[512]{0:T(512)S(1)} all-reduce(f32[512]{0:T(512)S(1)} %get-tuple-element.108), channel_id=1, replica_groups=mesh['seq'=8,'head'=4] {'head'}, use_global_device_ids=true, to_apply=%region_3.4 | all-reduce | flops 512 | bytes 4096 | tf_op jit(solution)/shard_map/psum | solution.py:60
  81.8 14.8 %all-gather.5.cloned.1.call-done = bf16[512,2048]{1,0:T(8,128)(2,1)} async-done(((bf16[512,512]{1,0:T(8,128)(2,1)}), bf16[512,2048]{1,0:T(8,128)(2,1)}) %all-gather.5.cloned.1.call-update) | async-done | bytes 2097168 | tf_op jit(solution)/shard_map/all_gather | solution.py:61
  96.6 75.0 %all-gather.7.cloned.1.call-done = bf16[2048,1024]{1,0:T(8,128)(2,1)} async-done(((bf16[256,1024]{1,0:T(8,128)(2,1)}), bf16[2048,1024]{1,0:T(8,128)(2,1)}) %all-gather.7.cloned.1.call-update) | async-done | bytes 4194320 | tf_op jit(solution)/shard_map/all_gather | solution.py:62
  171.6 6.1 %multiply_convert_fusion = bf16[512,1024]{1,0:T(8,128)(2,1)} fusion(bf16[512,2048]{1,0:T(8,128)(2,1)} %all-gather.5.cloned.1.call-done, bf16[2048,1024]{1,0:T(8,128)(2,1)} %all-gather.7.cloned.1.call-done, f32[512]{0:T(512)S(1)} %add_rsqrt_fusion), kind=kOutput, calls=%fused_computation.2 | convolution fusion | flops 2148532224 | bytes 7342080 | tf_op jit(solution)/shard_map/dot_general | solution.py:63
  (2 shorter events, 0.0 us)
Async XLA Ops:
  6.5 63.9 %copy-start = (bf16[512,512]{1,0:T(8,128)(2,1)S(1)}, bf16[512,512]{1,0:T(8,128)(2,1)}, u32[]{:S(2)}) copy-start(bf16[512,512]{1,0:T(8,128)(2,1)} %param.7) | copy-start | bytes 1572868
  6.5 55.3 %all-gather.9.cloned.1.call-start = ((), (), s32[]{:S(2)}) async-start(), calls=%async_computation.2 | async-start | bytes 2359296 | tf_op jit(solution)/shard_map/all_gather | solution.py:11
  9.9 86.7 %all-gather.5.cloned.1.call-start = ((), (), s32[]{:S(2)}) async-start(), calls=%async_computation | async-start | bytes 2621440 | tf_op jit(solution)/shard_map/all_gather | solution.py:61
  73.2 1.0 copy-start.1
  75.3 96.2 %all-gather.7.cloned.1.call-start = ((), (), s32[]{:S(2)}) async-start(), calls=%async_computation.1 | async-start | bytes 4718592 | tf_op jit(solution)/shard_map/all_gather | solution.py:62
Sparse Core Ops, SparseCore 0:
  10.0 51.7 all-gather.8
  75.5 21.0 all-gather.4
  98.7 72.7 all-gather.6
where the time goes:
time: 185 us; the launch traced here: 184 us
  waiting for transfers between devices  142 us (77%)
  between operations  13.2 us (7%)
  matrix products  10.9 us (6%)
  other arithmetic  9.53 us (5%)
  blocking collectives  5.67 us (3%)
  local copies, waits for them, and re-layouts  2.34 us (1%)
    all_gather x1, waiting for transfers between devices, per_device(): full_block = lax.all_gather(out_weight, 'seq', axis=0, tiled=True)  75 us
    all_gather x1, waiting for transfers between devices, carried_in(): everything = lax.all_gather(shard, axis)  51.8 us
    all_gather x1, waiting for transfers between devices, per_device(): features = lax.all_gather(hidden, 'head', axis=1, tiled=True)  14.8 us
    select_n x8, other arithmetic, turn(): return jnp.where(reached, new, before)  8.32 us
    dot_general x1, matrix products, per_device(): jnp.dot(features, full_block, preferred_element_type=jnp.float32)  6.12 us
    psum x1, blocking collectives, per_device(): total = lax.psum(squares, 'head')  5.67 us
  transfers between devices with their start and end apart: 3, of which 3 were waited for; matrix products, arithmetic and copies ran while one was open for 0% of the time, Pallas kernels for 0%

commit v1 on v0

v1 whole, which is shorter than its diff:
```python
import functools

import jax
import jax.numpy as jnp
from jax import lax
from jax.experimental import pallas as pl
from jax.experimental.pallas import tpu as pltpu
from jax.sharding import PartitionSpec as P

HD = 128
PIECES = 2
LONGEST_LINE = 8
MESH = pl.DeviceIdType.MESH
F32 = jnp.float32
BF16 = jnp.bfloat16


def dot(a, b, dims):
    return lax.dot_general(a, b, (dims, ((), ())), preferred_element_type=F32)


def fused_kernel(
    n, m,
    q_hbm, k_hbm, v_hbm, g_hbm, w_hbm, out_ref,
    q_ref, k_ref, v_ref, g_ref, w_all, hid, attn, own_state, s_out, s_in, t_out, t_in, prefix,
    sq, acc,
    load_sem, w_recv, up_send, down_send, side_send,
    s_send, s_recv, t_send, t_recv, h_send, h_recv, q_send, q_recv,
):
    rows, width = q_ref.shape
    heads = width // HD
    scale = HD ** (-0.5)
    depth = w_all.shape[1]
    piece = depth // PIECES
    per_peer = width // depth
    line = n // 2
    me = lax.axis_index("seq")
    hx = lax.axis_index("head")
    z = me // 2
    y = me % 2
    partner = z * 2 + (1 - y)

    loads = [
        pltpu.make_async_copy(src, dst, load_sem.at[i])
        for i, (src, dst) in enumerate(
            ((k_hbm, k_ref), (v_hbm, v_ref), (w_hbm, w_all.at[me]), (q_hbm, q_ref), (g_hbm, g_ref))
        )
    ]
    for load in loads:
        load.start()

    barrier = pltpu.get_barrier_semaphore()
    for d in range(1, line):
        other = ((z + d) % line) * 2 + y
        pl.semaphore_signal(barrier, inc=1, device_id={"seq": other}, device_id_type=MESH)
    pl.semaphore_signal(barrier, inc=1, device_id={"seq": partner}, device_id_type=MESH)
    for d in range(1, m):
        pl.semaphore_signal(barrier, inc=1, device_id={"head": (hx + d) % m}, device_id_type=MESH)

    def w_copy(block, c, send_sems, target):
        part = w_all.at[block, pl.ds(c * piece, piece), :]
        return pltpu.make_async_remote_copy(
            src_ref=part, dst_ref=part,
            send_sem=send_sems.at[block, c], recv_sem=w_recv.at[block, c],
            device_id={"seq": target}, device_id_type=MESH,
        )

    def up(block, c):
        return w_copy(block, c, up_send, jnp.minimum(me + 2, n - 1))

    def down(block, c):
        return w_copy(block, c, down_send, jnp.maximum(me - 2, 0))

    def side(block, c):
        return w_copy(block, c, side_send, partner)

    has_up = z < line - 1
    has_down = z > 0

    loads[0].wait()
    loads[1].wait()
    for h in range(heads):
        cols = slice(h * HD, (h + 1) * HD)
        state = dot(k_ref[:, cols], v_ref[:, cols], ((0,), (0,)))
        own_state[cols, :] = state
        s_out[cols, :] = state.astype(BF16)
    loads[2].wait()
    pl.semaphore_wait(barrier, line - 1 + 1 + m - 1)

    s_copy = pltpu.make_async_remote_copy(
        src_ref=s_out, dst_ref=s_in, send_sem=s_send, recv_sem=s_recv,
        device_id={"seq": partner}, device_id_type=MESH,
    )
    s_copy.start()

    @pl.when(has_down)
    def _():
        for c in range(PIECES):
            down(me, c).start()

    @pl.when(has_up)
    def _():
        up(me, 0).start()

    for c in range(PIECES):
        side(me, c).start()

    loads[3].wait()

    def local_head(h):
        cols = slice(h * HD, (h + 1) * HD)
        kh = k_ref[:, cols]
        vh = v_ref[:, cols]
        half = rows // 2
        for r in range(2):
            upto = (r + 1) * half
            scores = dot(q_ref[r * half:upto, cols], kh[:upto], ((1,), (1,))) * scale
            rowpos = r * half + lax.broadcasted_iota(jnp.int32, (half, upto), 0)
            colpos = lax.broadcasted_iota(jnp.int32, (half, upto), 1)
            scores = jnp.where(colpos <= rowpos, scores, 0.0).astype(BF16)
            attn[r * half:upto, cols] = dot(scores, vh[:upto], ((1,), (0,)))

    local_head(0)

    s_copy.wait_recv()
    t_out[...] = (own_state[...] + s_in[...].astype(F32)).astype(BF16)

    def t_copy(source, target):
        return pltpu.make_async_remote_copy(
            src_ref=t_out, dst_ref=t_in.at[source],
            send_sem=t_send.at[target], recv_sem=t_recv.at[source],
            device_id={"seq": target * 2 + y}, device_id_type=MESH,
        )

    for target in range(line - 1, 0, -1):
        @pl.when(target > z)
        def _():
            t_copy(z, target).start()

    @pl.when(has_up)
    def _():
        for c in range(1, PIECES):
            up(me, c).start()

    for h in range(1, heads):
        local_head(h)
    prefix[...] = jnp.where(y == 1, s_in[...].astype(F32), 0.0)

    def pass_down(step, c):
        @pl.when(z + step <= line - 1)
        def _():
            block = me + 2 * step
            side(block, c).wait_recv()

            @pl.when(has_down)
            def _():
                down(block, c).start()
            side(block, c).start()

    def pass_up(step, c):
        @pl.when(z >= step)
        def _():
            block = me - 2 * step
            side(block, c).wait_recv()

            @pl.when(has_up)
            def _():
                up(block, c).start()
            side(block, c).start()

    pass_down(1, 0)

    for source in range(line - 1):
        @pl.when(source < z)
        def _():
            t_copy(source, z).wait_recv()
            prefix[...] += t_in[source].astype(F32)

    loads[4].wait()
    total = jnp.zeros((rows, 1), F32)
    for h in range(heads):
        cols = slice(h * HD, (h + 1) * HD)
        inter = dot(q_ref[:, cols], prefix[cols, :].astype(BF16), ((1,), (0,))) * scale
        value = attn[:, cols] + inter
        total = total + jnp.sum(value * value, axis=1, keepdims=True)
        gate = g_ref[:, cols].astype(F32)
        gated = (value * (gate / (1.0 + jnp.exp(-gate)))).astype(BF16)
        block, offset = divmod(h * HD, depth)
        hid[hx * per_peer + block, :, offset:offset + HD] = gated
    sq[hx] = jnp.broadcast_to(total, (rows, HD)).T[:8]

    peers = [(hx + d) % m for d in range(1, m)]

    def h_copy(d):
        part = hid.at[pl.ds(hx * per_peer, per_peer)]
        return pltpu.make_async_remote_copy(
            src_ref=part, dst_ref=part, send_sem=h_send.at[d], recv_sem=h_recv.at[hx],
            device_id={"head": peers[d]}, device_id_type=MESH,
        )

    def q_copy(d):
        return pltpu.make_async_remote_copy(
            src_ref=sq.at[hx], dst_ref=sq.at[hx], send_sem=q_send.at[d], recv_sem=q_recv.at[hx],
            device_id={"head": peers[d]}, device_id_type=MESH,
        )

    for d in range(m - 1):
        q_copy(d).start()
        h_copy(d).start()

    for c in range(1, PIECES):
        pass_down(1, c)
    for c in range(PIECES):
        pass_up(1, c)
    for step in range(2, line):
        for c in range(PIECES):
            pass_down(step, c)
            pass_up(step, c)

    for d in range(m - 1):
        source = peers[d]
        part = hid.at[pl.ds(source * per_peer, per_peer)]
        pltpu.make_async_remote_copy(
            src_ref=part, dst_ref=part, send_sem=h_send.at[d], recv_sem=h_recv.at[source],
            device_id={"head": source}, device_id_type=MESH,
        ).wait_recv()
        pltpu.make_async_remote_copy(
            src_ref=sq.at[source], dst_ref=sq.at[source], send_sem=q_send.at[d],
            recv_sem=q_recv.at[source], device_id={"head": source}, device_id_type=MESH,
        ).wait_recv()
    squares = sq[0]
    for i in range(1, m):
        squares = squares + sq[i]
    inverse = lax.rsqrt(squares / (m * width) + 1e-06)
    inverse = jnp.broadcast_to(inverse[:1], (HD, rows)).T[:, :1]

    acc[...] = jnp.zeros_like(acc)
    low = z < line // 2

    def place(j):
        return jnp.where(low, (z + j) % line, (z + line - j) % line)

    def own_column(j, carry):
        block = place(j) * 2 + y
        acc[...] += dot(hid[block], w_all[block], ((1,), (0,)))
        return carry

    lax.fori_loop(0, line, own_column, 0)

    def other_column(j, carry):
        block = place(j) * 2 + (1 - y)
        for c in range(PIECES):
            side(block, c).wait_recv()
        acc[...] += dot(hid[block], w_all[block], ((1,), (0,)))
        return carry

    lax.fori_loop(0, line, other_column, 0)
    out_ref[...] = (acc[...] * inverse).astype(out_ref.dtype)

    s_copy.wait_send()
    for target in range(1, line):
        @pl.when(target > z)
        def _():
            t_copy(z, target).wait_send()
    for d in range(m - 1):
        h_copy(d).wait_send()
        q_copy(d).wait_send()
    for zb in range(line):
        block = zb * 2 + y

        @pl.when((zb <= z) & has_up)
        def _():
            for c in range(PIECES):
                up(block, c).wait_send()

        @pl.when((zb >= z) & has_down)
        def _():
            for c in range(PIECES):
                down(block, c).wait_send()
        for c in range(PIECES):
            side(block, c).wait_send()


def fused(n, m, queries, key_vectors, value_vectors, gate_input, out_weight):
    rows, width = queries.shape
    depth, columns = out_weight.shape
    line = n // 2
    dma = pltpu.SemaphoreType.DMA
    return pl.pallas_call(
        functools.partial(fused_kernel, n, m),
        out_shape=jax.ShapeDtypeStruct((rows, columns), BF16),
        in_specs=[pl.BlockSpec(memory_space=pl.ANY)] * 5,
        out_specs=pl.BlockSpec(memory_space=pltpu.VMEM),
        scratch_shapes=[
            pltpu.VMEM((rows, width), BF16),
            pltpu.VMEM((rows, width), BF16),
            pltpu.VMEM((rows, width), BF16),
            pltpu.VMEM((rows, width), BF16),
            pltpu.VMEM((n, depth, columns), BF16),
            pltpu.VMEM((n, rows, depth), BF16),
            pltpu.VMEM((rows, width), F32),
            pltpu.VMEM((width, HD), F32),
            pltpu.VMEM((width, HD), BF16),
            pltpu.VMEM((width, HD), BF16),
            pltpu.VMEM((width, HD), BF16),
            pltpu.VMEM((line, width, HD), BF16),
            pltpu.VMEM((width, HD), F32),
            pltpu.VMEM((m, 8, rows), F32),
            pltpu.VMEM((rows, columns), F32),
            dma((5,)),
            dma((n, PIECES)),
            dma((n, PIECES)),
            dma((n, PIECES)),
            dma((n, PIECES)),
            dma,
            dma,
            dma((line,)),
            dma((line,)),
            dma((m,)),
            dma((m,)),
            dma((m,)),
            dma((m,)),
        ],
        compiler_params=pltpu.CompilerParams(
            collective_id=0, has_side_effects=True, vmem_limit_bytes=48 * 1024 * 1024
        ),
        cost_estimate=pl.CostEstimate(
            flops=2 * rows * n * depth * columns, bytes_accessed=2 * n * depth * columns,
            transcendentals=rows * width,
        ),
    )(queries, key_vectors, value_vectors, gate_input, out_weight)


def long_line(queries, key_vectors, value_vectors, gate_input, out_weight):
    rows, width = queries.shape
    heads = width // HD
    scale = HD ** (-0.5)
    qhead = queries.reshape(rows, heads, HD)
    khead = key_vectors.reshape(rows, heads, HD)
    vhead = value_vectors.reshape(rows, heads, HD)
    own_state = jnp.einsum("thd,the->hde", khead, vhead, preferred_element_type=F32)
    scores = jnp.einsum("thd,shd->hts", qhead, khead, preferred_element_type=F32) * scale
    rowpos = lax.broadcasted_iota(jnp.int32, (rows, rows), 0)
    colpos = lax.broadcasted_iota(jnp.int32, (rows, rows), 1)
    scores = jnp.where((colpos <= rowpos)[None, :, :], scores, 0.0).astype(BF16)
    local = jnp.einsum("hts,she->the", scores, vhead, preferred_element_type=F32)
    states = lax.all_gather(own_state, "seq")
    position = lax.axis_index("seq")

    def turn(k, before):
        return jnp.where(k < position, before + states[k], before)

    prefix = lax.fori_loop(0, lax.axis_size("seq"), turn, jnp.zeros_like(own_state))
    inter = jnp.einsum("thd,hde->the", qhead, prefix.astype(BF16), preferred_element_type=F32)
    attn = (local + inter * scale).reshape(rows, width)
    total = lax.psum(jnp.sum(attn * attn, axis=1), "head")
    hidden = (attn * jax.nn.silu(gate_input.astype(F32))).astype(BF16)
    features = lax.all_gather(hidden, "head", axis=1, tiled=True)
    weights = lax.all_gather(out_weight, "seq", axis=0, tiled=True)
    projected = jnp.dot(features, weights, preferred_element_type=F32)
    mean_square = total / features.shape[1]
    return (projected * lax.rsqrt(mean_square + 1e-06)[:, None]).astype(BF16)


def solution(mesh):
    n, m = mesh.shape["seq"], mesh.shape["head"]

    def per_device(queries, key_vectors, value_vectors, gate_input, out_weight):
        args = (queries, key_vectors, value_vectors, gate_input, out_weight)
        width, depth = queries.shape[1], out_weight.shape[0]
        short = n % 2 == 0 and n // 2 <= LONGEST_LINE
        if short and width % depth == 0 and depth % HD == 0:
            return fused(n, m, *args)
        return long_line(*args)

    placed = (P("seq", "head"),) * 5
    return jax.shard_map(
        per_device, mesh=mesh, in_specs=placed, out_specs=P("seq", "head"), check_vma=False
    )
```

time: 185 us -> 63 us (0.34)
  waiting for transfers between devices: 142 us -> 0 us
  Pallas kernels: 0 us -> 56.4 us
  between operations: 13.2 us -> 0.01 us
  matrix products: 10.9 us -> 0 us
  other arithmetic: 9.53 us -> 0 us
  blocking collectives: 5.67 us -> 0 us
  local copies, waits for them, and re-layouts: 2.34 us -> 6.18 us
    all_gather x3 -> x0, waiting for transfers between devices: 142 us -> none  [the longest x1 75 us: per_device(): full_block = lax.all_gather(out_weight, 'seq', axis=0, tiled=True)]
    pallas_call x0 -> x1, Pallas kernels: none -> 56.4 us  [fused(): pl.pallas_call(functools.partial(fused_kernel, n, m), out_shape=jax.Shape...]
    dot_general x4 -> x0, matrix products: 10.9 us -> none  [the longest x1 6.12 us: per_device(): jnp.dot(features, full_block, preferred_element_type=jnp.float32)]
    select_n x8 -> x0, other arithmetic: 8.32 us -> none  [turn(): return jnp.where(reached, new, before)]
    psum x1 -> x0, blocking collectives: 5.67 us -> none  [per_device(): total = lax.psum(squares, 'head')]
    unnamed x4 -> x11, local copies, waits for them, and re-layouts: 0.7 us -> 6.18 us
  transfers between devices with their start and end apart: 3 -> 0, of which waited for: 3 -> 0; matrix products, arithmetic and copies ran while one was open for 0% -> 0% of each run, Pallas kernels for 0% -> 0%
where the time goes in v1:
time: 63 us; the launch traced here: 62.6 us
  Pallas kernels  56.4 us (90%)
  local copies, waits for them, and re-layouts  6.18 us (10%)
    pallas_call x1, Pallas kernels, fused(): pl.pallas_call(functools.partial(fused_kernel, n, m), out_shape=jax.Shape...  56.4 us
    unnamed x11, local copies, waits for them, and re-layouts  6.18 us

profile of v1, /device:TPU:0, one launch (start us, length us, event | category | flops | bytes accessed | tf_op | source)
XLA Modules:
  0.0 62.6 jit_solution(602842135767597664)
XLA Ops:
  0.0 0.0 copy-start
  0.0 1.0 %copy-done = bf16[512,512]{1,0:T(8,128)(2,1)S(1)} copy-done((bf16[512,512]{1,0:T(8,128)(2,1)S(1)}, bf16[512,512]{1,0:T(8,128)(2,1)}, u32[]{:S(2)}) %copy-start) | copy-done | bytes 524312
  1.0 0.0 copy-start.1
  1.0 1.0 %copy-done.1 = bf16[512,512]{1,0:T(8,128)(2,1)S(1)} copy-done((bf16[512,512]{1,0:T(8,128)(2,1)S(1)}, bf16[512,512]{1,0:T(8,128)(2,1)}, u32[]{:S(2)}) %copy-start.1) | copy-done | bytes 524312
  2.1 0.0 copy-start.2
  2.1 1.0 %copy-done.2 = bf16[512,512]{1,0:T(8,128)(2,1)S(1)} copy-done((bf16[512,512]{1,0:T(8,128)(2,1)S(1)}, bf16[512,512]{1,0:T(8,128)(2,1)}, u32[]{:S(2)}) %copy-start.2) | copy-done | bytes 524312
  3.1 0.0 copy-start.3
  3.1 1.0 %copy-done.3 = bf16[512,512]{1,0:T(8,128)(2,1)S(1)} copy-done((bf16[512,512]{1,0:T(8,128)(2,1)S(1)}, bf16[512,512]{1,0:T(8,128)(2,1)}, u32[]{:S(2)}) %copy-start.3) | copy-done | bytes 524312
  4.2 0.0 copy-start.4
  4.2 1.0 %copy-done.4 = bf16[256,1024]{1,0:T(8,128)(2,1)S(1)} copy-done((bf16[256,1024]{1,0:T(8,128)(2,1)S(1)}, bf16[256,1024]{1,0:T(8,128)(2,1)}, u32[]{:S(2)}) %copy-start.4) | copy-done | bytes 524312
  5.2 56.4 %shard_map.55 = bf16[512,1024]{1,0:T(8,128)(2,1)S(1)} custom-call(bf16[512,512]{1,0:T(8,128)(2,1)S(1)} %copy-done, bf16[512,512]{1,0:T(8,128)(2,1)S(1)} %copy-done.1, bf16[512,512]{1,0:T(8,128)(2,1)S(1)} %copy-done.2, bf16[512,512]{1,0:T(8,128)(2,1)S(1)} %copy-done.3, bf16[256,1024]{1,0:T(8,128)(2,1)S(1)} %copy-done.4), custom_call_target="tpu_custom_call" | custom-call | flops 2147483648 | bytes 4194304 | tf_op jit(solution)/shard_map/pallas_call | solution.py:289
  61.7 1.0 %copy.7 = bf16[512,1024]{1,0:T(8,128)(2,1)} copy(bf16[512,1024]{1,0:T(8,128)(2,1)S(1)} %shard_map.55) | data formatting | bytes 2097152
Async XLA Ops:
  0.0 1.0 %copy-start = (bf16[512,512]{1,0:T(8,128)(2,1)S(1)}, bf16[512,512]{1,0:T(8,128)(2,1)}, u32[]{:S(2)}) copy-start(bf16[512,512]{1,0:T(8,128)(2,1)} %q_hbm.1) | copy-start | bytes 1572868
  1.0 1.0 %copy-start.1 = (bf16[512,512]{1,0:T(8,128)(2,1)S(1)}, bf16[512,512]{1,0:T(8,128)(2,1)}, u32[]{:S(2)}) copy-start(bf16[512,512]{1,0:T(8,128)(2,1)} %k_hbm.1) | copy-start | bytes 1572868
  2.1 1.0 %copy-start.2 = (bf16[512,512]{1,0:T(8,128)(2,1)S(1)}, bf16[512,512]{1,0:T(8,128)(2,1)}, u32[]{:S(2)}) copy-start(bf16[512,512]{1,0:T(8,128)(2,1)} %v_hbm.1) | copy-start | bytes 1572868
  3.1 1.0 %copy-start.3 = (bf16[512,512]{1,0:T(8,128)(2,1)S(1)}, bf16[512,512]{1,0:T(8,128)(2,1)}, u32[]{:S(2)}) copy-start(bf16[512,512]{1,0:T(8,128)(2,1)} %g_hbm.1) | copy-start | bytes 1572868
  4.2 1.0 %copy-start.4 = (bf16[256,1024]{1,0:T(8,128)(2,1)S(1)}, bf16[256,1024]{1,0:T(8,128)(2,1)}, u32[]{:S(2)}) copy-start(bf16[256,1024]{1,0:T(8,128)(2,1)} %w_hbm.1) | copy-start | bytes 1572868

commit v2 on v1

--- a/solution.py
+++ b/solution.py
@@ -8,7 +8,9 @@
 from jax.sharding import PartitionSpec as P
 
 HD = 128
-PIECES = 2
+PIECES = 4
+CROSS_DOWN = 1
+CROSS_UP = 0
 LONGEST_LINE = 8
 MESH = pl.DeviceIdType.MESH
 F32 = jnp.float32
@@ -43,15 +45,16 @@
     loads = [
         pltpu.make_async_copy(src, dst, load_sem.at[i])
         for i, (src, dst) in enumerate(
-            ((k_hbm, k_ref), (v_hbm, v_ref), (w_hbm, w_all.at[me]), (q_hbm, q_ref), (g_hbm, g_ref))
+            ((w_hbm, w_all.at[me]), (k_hbm, k_ref), (v_hbm, v_ref), (q_hbm, q_ref), (g_hbm, g_ref))
         )
     ]
     for load in loads:
         load.start()
 
     barrier = pltpu.get_barrier_semaphore()
-    for d in range(1, line):
-        other = ((z + d) % line) * 2 + y
+    above = jnp.where(z == line - 1, y, me + 2)
+    below = jnp.where(z == 0, n - 2 + y, me - 2)
+    for other in (above, below):
         pl.semaphore_signal(barrier, inc=1, device_id={"seq": other}, device_id_type=MESH)
     pl.semaphore_signal(barrier, inc=1, device_id={"seq": partner}, device_id_type=MESH)
     for d in range(1, m):
@@ -74,35 +77,48 @@
     def side(block, c):
         return w_copy(block, c, side_send, partner)
 
+    order = tuple(reversed(range(PIECES)))
+    cross_down, cross_up = order[:CROSS_DOWN], order[:CROSS_UP]
+    crossing = order[:max(CROSS_DOWN, CROSS_UP)]
     has_up = z < line - 1
     has_down = z > 0
 
+    early = PIECES // 2
+    ahead = PIECES // 4
     loads[0].wait()
+    pl.semaphore_wait(barrier, 3 + m - 1)
+    for c in order[:ahead]:
+        side(me, c).start()
+
+    @pl.when(has_down)
+    def _():
+        for c in order:
+            down(me, c).start()
+
+    @pl.when(has_up)
+    def _():
+        for c in order[:early]:
+            up(me, c).start()
+
+    @pl.when(has_up & has_down)
+    def _():
+        for c in order[early:]:
+            up(me, c).start()
+
     loads[1].wait()
+    loads[2].wait()
     for h in range(heads):
         cols = slice(h * HD, (h + 1) * HD)
         state = dot(k_ref[:, cols], v_ref[:, cols], ((0,), (0,)))
         own_state[cols, :] = state
         s_out[cols, :] = state.astype(BF16)
-    loads[2].wait()
-    pl.semaphore_wait(barrier, line - 1 + 1 + m - 1)
 
     s_copy = pltpu.make_async_remote_copy(
         src_ref=s_out, dst_ref=s_in, send_sem=s_send, recv_sem=s_recv,
         device_id={"seq": partner}, device_id_type=MESH,
     )
     s_copy.start()
-
-    @pl.when(has_down)
-    def _():
-        for c in range(PIECES):
-            down(me, c).start()
-
-    @pl.when(has_up)
-    def _():
-        up(me, 0).start()
-
-    for c in range(PIECES):
+    for c in order[ahead:]:
         side(me, c).start()
 
     loads[3].wait()
@@ -123,58 +139,84 @@
     local_head(0)
 
     s_copy.wait_recv()
-    t_out[...] = (own_state[...] + s_in[...].astype(F32)).astype(BF16)
-
-    def t_copy(source, target):
-        return pltpu.make_async_remote_copy(
-            src_ref=t_out, dst_ref=t_in.at[source],
-            send_sem=t_send.at[target], recv_sem=t_recv.at[source],
-            device_id={"seq": target * 2 + y}, device_id_type=MESH,
-        )
-
-    for target in range(line - 1, 0, -1):
-        @pl.when(target > z)
-        def _():
-            t_copy(z, target).start()
-
-    @pl.when(has_up)
-    def _():
-        for c in range(1, PIECES):
+    t_copy = pltpu.make_async_remote_copy(
+        src_ref=t_out, dst_ref=t_in, send_sem=t_send, recv_sem=t_recv,
+        device_id={"seq": jnp.minimum(me + 2, n - 1)}, device_id_type=MESH,
+    )
+
+    @pl.when(z == 0)
+    def _():
+        t_out[...] = (own_state[...] + s_in[...].astype(F32)).astype(BF16)
+        t_copy.start()
+        for c in order[early:]:
             up(me, c).start()
 
     for h in range(1, heads):
         local_head(h)
     prefix[...] = jnp.where(y == 1, s_in[...].astype(F32), 0.0)
 
-    def pass_down(step, c):
+    def pass_down(step, c, own):
         @pl.when(z + step <= line - 1)
         def _():
-            block = me + 2 * step
+            block = (z + step) * 2 + (y if own else 1 - y)
             side(block, c).wait_recv()
 
             @pl.when(has_down)
             def _():
                 down(block, c).start()
-            side(block, c).start()
-
-    def pass_up(step, c):
+            if c not in cross_down:
+                side(block, c).start()
+
+    def pass_up(step, c, own):
         @pl.when(z >= step)
         def _():
-            block = me - 2 * step
+            block = (z - step) * 2 + (y if own else 1 - y)
             side(block, c).wait_recv()
 
             @pl.when(has_up)
             def _():
                 up(block, c).start()
-            side(block, c).start()
-
-    pass_down(1, 0)
-
-    for source in range(line - 1):
-        @pl.when(source < z)
+            if c not in cross_up:
+                side(block, c).start()
+
+    def turn_off(c):
+        side(partner, c).wait_recv()
+        if c in cross_down:
+            @pl.when(has_down)
+            def _():
+                down(partner, c).start()
+        if c in cross_up:
+            @pl.when(has_up)
+            def _():
+                up(partner, c).start()
+
+    def pass_both(step, c):
+        pass_down(step, c, True)
+        pass_up(step, c, True)
+        if c in cross_down:
+            pass_down(step, c, False)
+        if c in cross_up:
+            pass_up(step, c, False)
+
+    for c in order[:early]:
+        pass_down(1, c, True)
+
+    @pl.when(z >= 2)
+    def _():
+        for c in order[:ahead]:
+            pass_up(1, c, True)
+
+    @pl.when(has_down)
+    def _():
+        t_copy.wait_recv()
+
+        @pl.when(has_up)
         def _():
-            t_copy(source, z).wait_recv()
-            prefix[...] += t_in[source].astype(F32)
+            t_out[...] = (
+                t_in[...].astype(F32) + own_state[...] + s_in[...].astype(F32)
+            ).astype(BF16)
+            t_copy.start()
+        prefix[...] += t_in[...].astype(F32)
 
     loads[4].wait()
     total = jnp.zeros((rows, 1), F32)
@@ -191,94 +233,126 @@
 
     peers = [(hx + d) % m for d in range(1, m)]
 
-    def h_copy(d):
-        part = hid.at[pl.ds(hx * per_peer, per_peer)]
+    mate = hx + 1 - 2 * (hx % 2)
+    pairs = m // 2
+
+    def h_copy(source, target, i):
+        part = hid.at[pl.ds(source * per_peer, per_peer)]
         return pltpu.make_async_remote_copy(
-            src_ref=part, dst_ref=part, send_sem=h_send.at[d], recv_sem=h_recv.at[hx],
-            device_id={"head": peers[d]}, device_id_type=MESH,
+            src_ref=part, dst_ref=part, send_sem=h_send.at[i], recv_sem=h_recv.at[source],
+            device_id={"head": target}, device_id_type=MESH,
         )
 
-    def q_copy(d):
+    def q_copy(source, d):
         return pltpu.make_async_remote_copy(
-            src_ref=sq.at[hx], dst_ref=sq.at[hx], send_sem=q_send.at[d], recv_sem=q_recv.at[hx],
-            device_id={"head": peers[d]}, device_id_type=MESH,
+            src_ref=sq.at[source], dst_ref=sq.at[source], send_sem=q_send.at[d],
+            recv_sem=q_recv.at[source], device_id={"head": peers[d]}, device_id_type=MESH,
         )
 
+    h_sends = [h_copy(hx, (hx + 2 * d) % m, d) for d in range(1, pairs)] + [h_copy(hx, mate, 0)]
+    q_sends = [q_copy(hx, d) for d in range(m - 1)]
+    for send in q_sends + h_sends:
+        send.start()
+
+    for c in crossing:
+        turn_off(c)
+
+    @pl.when(z < 2)
+    def _():
+        for c in order[:ahead]:
+            pass_up(1, c, True)
+    for c in order[ahead:early]:
+        pass_up(1, c, True)
+    for c in order[early:]:
+        pass_down(1, c, True)
+        pass_up(1, c, True)
+    for c in cross_down:
+        pass_down(1, c, False)
+    for c in cross_up:
+        pass_up(1, c, False)
+    for step in range(2, line - 1):
+        for c in order:
+            pass_both(step, c)
+
+    relays = []
+    for d in range(1, pairs):
+        source = (hx + 2 * d) % m
+        relay = h_copy(source, mate, pairs + d)
+        relay.wait_recv()
+        relay.start()
+        relays.append(relay)
+    for d in range(pairs):
+        h_copy((mate + 2 * d) % m, mate, 0).wait_recv()
     for d in range(m - 1):
-        q_copy(d).start()
-        h_copy(d).start()
-
-    for c in range(1, PIECES):
-        pass_down(1, c)
-    for c in range(PIECES):
-        pass_up(1, c)
-    for step in range(2, line):
-        for c in range(PIECES):
-            pass_down(step, c)
-            pass_up(step, c)
-
-    for d in range(m - 1):
-        source = peers[d]
-        part = hid.at[pl.ds(source * per_peer, per_peer)]
-        pltpu.make_async_remote_copy(
-            src_ref=part, dst_ref=part, send_sem=h_send.at[d], recv_sem=h_recv.at[source],
-            device_id={"head": source}, device_id_type=MESH,
-        ).wait_recv()
-        pltpu.make_async_remote_copy(
-            src_ref=sq.at[source], dst_ref=sq.at[source], send_sem=q_send.at[d],
-            recv_sem=q_recv.at[source], device_id={"head": source}, device_id_type=MESH,
-        ).wait_recv()
+        q_copy(peers[d], d).wait_recv()
     squares = sq[0]
     for i in range(1, m):
         squares = squares + sq[i]
     inverse = lax.rsqrt(squares / (m * width) + 1e-06)
     inverse = jnp.broadcast_to(inverse[:1], (HD, rows)).T[:, :1]
 
-    acc[...] = jnp.zeros_like(acc)
-    low = z < line // 2
+    near = jnp.minimum(z, line - 1 - z)
 
     def place(j):
-        return jnp.where(low, (z + j) % line, (z + line - j) % line)
-
-    def own_column(j, carry):
-        block = place(j) * 2 + y
+        d = (j + 1) // 2
+        alternate = z + d if j % 2 else z - d
+        beyond = jnp.where(z < line // 2, j, line - 1 - j)
+        return jnp.where(j <= 2 * near, alternate, beyond)
+
+    def wait_side(zb):
+        block = zb * 2 + (1 - y)
+        for where, crossed in ((zb > z, cross_down), (zb == z, crossing), (zb < z, cross_up)):
+            @pl.when(where)
+            def _():
+                for c in order:
+                    if c not in crossed:
+                        side(block, c).wait_recv()
+
+    def add_block(block):
         acc[...] += dot(hid[block], w_all[block], ((1,), (0,)))
-        return carry
-
-    lax.fori_loop(0, line, own_column, 0)
-
-    def other_column(j, carry):
+
+    block = me
+    acc[...] = dot(hid[block], w_all[block], ((1,), (0,)))
+    for j in range(1, line):
+        if j == line - 1:
+            for c in order[(line - 2) * ahead:]:
+                pass_both(line - 1, c)
+        else:
+            for c in order[(j - 1) * ahead:j * ahead]:
+                pass_both(line - 1, c)
+        add_block(place(j) * 2 + y)
+    for j in range(line):
         block = place(j) * 2 + (1 - y)
-        for c in range(PIECES):
-            side(block, c).wait_recv()
-        acc[...] += dot(hid[block], w_all[block], ((1,), (0,)))
-        return carry
-
-    lax.fori_loop(0, line, other_column, 0)
+        wait_side(place(j))
+        add_block(block)
     out_ref[...] = (acc[...] * inverse).astype(out_ref.dtype)
 
     s_copy.wait_send()
-    for target in range(1, line):
-        @pl.when(target > z)
-        def _():
-            t_copy(z, target).wait_send()
-    for d in range(m - 1):
-        h_copy(d).wait_send()
-        q_copy(d).wait_send()
+
+    @pl.when(has_up)
+    def _():
+        t_copy.wait_send()
+    for send in q_sends + h_sends + relays:
+        send.wait_send()
     for zb in range(line):
-        block = zb * 2 + y
-
-        @pl.when((zb <= z) & has_up)
-        def _():
-            for c in range(PIECES):
-                up(block, c).wait_send()
-
-        @pl.when((zb >= z) & has_down)
-        def _():
-            for c in range(PIECES):
-                down(block, c).wait_send()
-        for c in range(PIECES):
-            side(block, c).wait_send()
+        for column, ups, downs in ((y, order, order), (1 - y, cross_up, cross_down)):
+            block = zb * 2 + column
+
+            @pl.when((zb <= z) & has_up)
+            def _():
+                for c in ups:
+                    up(block, c).wait_send()
+
+            @pl.when((zb >= z) & has_down)
+            def _():
+                for c in downs:
+                    down(block, c).wait_send()
+        for where, crossed in ((zb > z, cross_down), (zb == z, ()), (zb < z, cross_up)):
+            @pl.when(where)
+            def _():
+                for c in order:
+                    if c not in crossed:
+                        side(zb * 2 + y, c).wait_send()
 
 
 def fused(n, m, queries, key_vectors, value_vectors, gate_input, out_weight):
@@ -289,7 +363,7 @@
     return pl.pallas_call(
         functools.partial(fused_kernel, n, m),
         out_shape=jax.ShapeDtypeStruct((rows, columns), BF16),
-        in_specs=[pl.BlockSpec(memory_space=pl.ANY)] * 5,
+        in_specs=[pl.BlockSpec(memory_space=pltpu.HBM)] * 5,
         out_specs=pl.BlockSpec(memory_space=pltpu.VMEM),
         scratch_shapes=[
             pltpu.VMEM((rows, width), BF16),
@@ -303,7 +377,7 @@
             pltpu.VMEM((width, HD), BF16),
             pltpu.VMEM((width, HD), BF16),
             pltpu.VMEM((width, HD), BF16),
-            pltpu.VMEM((line, width, HD), BF16),
+            pltpu.VMEM((width, HD), BF16),
             pltpu.VMEM((width, HD), F32),
             pltpu.VMEM((m, 8, rows), F32),
             pltpu.VMEM((rows, columns), F32),
@@ -314,15 +388,15 @@
             dma((n, PIECES)),
             dma,
             dma,
-            dma((line,)),
-            dma((line,)),
+            dma,
+            dma,
             dma((m,)),
             dma((m,)),
             dma((m,)),
             dma((m,)),
         ],
         compiler_params=pltpu.CompilerParams(
-            collective_id=0, has_side_effects=True, vmem_limit_bytes=48 * 1024 * 1024
+            collective_id=0, has_side_effects=True, vmem_limit_bytes=57000 * 1024
         ),
         cost_estimate=pl.CostEstimate(
             flops=2 * rows * n * depth * columns, bytes_accessed=2 * n * depth * columns,
@@ -368,7 +442,7 @@
     def per_device(queries, key_vectors, value_vectors, gate_input, out_weight):
         args = (queries, key_vectors, value_vectors, gate_input, out_weight)
         width, depth = queries.shape[1], out_weight.shape[0]
-        short = n % 2 == 0 and n // 2 <= LONGEST_LINE
+        short = n % 2 == 0 and m % 2 == 0 and 3 <= n // 2 <= LONGEST_LINE
         if short and width % depth == 0 and depth % HD == 0:
             return fused(n, m, *args)
         return long_line(*args)

time: 63 us -> 58.3 us (0.925)
  local copies, waits for them, and re-layouts: 6.18 us -> 2.26 us
    unnamed x11 -> x1, local copies, waits for them, and re-layouts: 6.18 us -> 2.26 us
where the time goes in v2:
time: 58.3 us; the launch traced here: 58.1 us
  Pallas kernels  55.8 us (96%)
  local copies, waits for them, and re-layouts  2.26 us (4%)
    pallas_call x1, Pallas kernels, fused(): pl.pallas_call(functools.partial(fused_kernel, n, m), out_shape=jax.Shape...  55.8 us
    unnamed x1, local copies, waits for them, and re-layouts  2.26 us

profile of v2, /device:TPU:0, one launch (start us, length us, event | category | flops | bytes accessed | tf_op | source)
XLA Modules:
  0.0 58.1 jit_solution(5134234678722834327)
XLA Ops:
  0.0 55.8 %shard_map.55 = bf16[512,1024]{1,0:T(8,128)(2,1)} custom-call(bf16[512,512]{1,0:T(8,128)(2,1)} %q_hbm.1, bf16[512,512]{1,0:T(8,128)(2,1)} %k_hbm.1, bf16[512,512]{1,0:T(8,128)(2,1)} %v_hbm.1, bf16[512,512]{1,0:T(8,128)(2,1)} %g_hbm.1, bf16[256,1024]{1,0:T(8,128)(2,1)} %w_hbm.1), custom_call_target="tpu_custom_call" | custom-call | flops 2147483648 | bytes 4194304 | tf_op jit(solution)/shard_map/pallas_call | solution.py:363
  55.8 2.3 %copy.7 = bf16[512,1024]{1,0:T(8,128)(2,1)} copy(bf16[512,1024]{1,0:T(8,128)(2,1)} %shard_map.55) | data formatting | bytes 2097152

commit v3 on v2

--- a/solution.py
+++ b/solution.py
@@ -203,7 +203,14 @@
 
     @pl.when(z >= 2)
     def _():
+        for c in order[early:]:
+            pass_down(1, c, True)
         for c in order[:ahead]:
+            pass_up(1, c, True)
+
+    @pl.when(z == line - 1)
+    def _():
+        for c in order[ahead:]:
             pass_up(1, c, True)
 
     @pl.when(has_down)
@@ -261,11 +268,13 @@
     def _():
         for c in order[:ahead]:
             pass_up(1, c, True)
-    for c in order[ahead:early]:
-        pass_up(1, c, True)
-    for c in order[early:]:
-        pass_down(1, c, True)
-        pass_up(1, c, True)
+        for c in order[early:]:
+            pass_down(1, c, True)
+
+    @pl.when(has_up)
+    def _():
+        for c in order[ahead:]:
+            pass_up(1, c, True)
     for c in cross_down:
         pass_down(1, c, False)
     for c in cross_up:

time: 58.3 us -> 59.8 us (1.026)
  Pallas kernels: 55.8 us -> 57.4 us
    pallas_call x1, Pallas kernels: 55.8 us -> 57.4 us  [fused(): pl.pallas_call(functools.partial(fused_kernel, n, m), out_shape=jax.Shape...]
where the time goes in v3:
time: 59.8 us; the launch traced here: 59.6 us
  Pallas kernels  57.4 us (96%)
  local copies, waits for them, and re-layouts  2.26 us (4%)
    pallas_call x1, Pallas kernels, fused(): pl.pallas_call(functools.partial(fused_kernel, n, m), out_shape=jax.Shape...  57.4 us
    unnamed x1, local copies, waits for them, and re-layouts  2.26 us

profile of v3, /device:TPU:0, one launch (start us, length us, event | category | flops | bytes accessed | tf_op | source)
XLA Modules:
  0.0 59.6 jit_solution(7645596991068632774)
XLA Ops:
  0.0 57.4 %shard_map.55 = bf16[512,1024]{1,0:T(8,128)(2,1)} custom-call(bf16[512,512]{1,0:T(8,128)(2,1)} %q_hbm.1, bf16[512,512]{1,0:T(8,128)(2,1)} %k_hbm.1, bf16[512,512]{1,0:T(8,128)(2,1)} %v_hbm.1, bf16[512,512]{1,0:T(8,128)(2,1)} %g_hbm.1, bf16[256,1024]{1,0:T(8,128)(2,1)} %w_hbm.1), custom_call_target="tpu_custom_call" | custom-call | flops 2147483648 | bytes 4194304 | tf_op jit(solution)/shard_map/pallas_call | solution.py:372
  57.4 2.3 %copy.7 = bf16[512,1024]{1,0:T(8,128)(2,1)} copy(bf16[512,1024]{1,0:T(8,128)(2,1)} %shard_map.55) | data formatting | bytes 2097152
